TPU v7x, 32 devices: a whole 2x2x4 slice. The times are simulated.
32 devices in a mesh: blk: 8 (over z, x), grp: 4 (over y, core).
Axes of the slice: x: 2, y: 2, z: 4, core: 2. Of those that a mesh axis runs over, the one named last changes fastest.
Arguments:
- amplitudes: bfloat16 [8, 512, 1024], P('blk', None, 'grp'), may hold values from -6 to 6
- integrals: bfloat16 [64, 1024, 1024], P('blk', 'grp'), may hold values from -0.1875 to 0.1875
- cd_index: int32 [64], replicated, may hold values from 0 to 7, as said below
- live_blocks: int32 [8], replicated, may hold values from 4 to 8, as said below
- occ_energy: float32 [512], P('grp'), may hold values from -3 to -0.5
- vir_energy: float32 [8, 1024], P('blk'), may hold values from 0.5 to 4
Outputs:
- amplitude_step: float32 [8, 512, 1024], P('blk', 'grp')
Inputs may be any that keep to these rules, and one draw needn't show every extreme that they name: (cd_index[k] - k // 8) mod 8 is at most 2 or at least 6; among the first 4 slots of each pair block every nonzero offset from -2 to 2 occurs once. `live_blocks`: 8 is reached by some pair block in every draw.
All inputs are finite; a program needn't handle non-finite values.
Results may differ from a plain program's by a relative error of at most 0.0003.
Values may be sent and summed in bfloat16 or wider, within the bound.
A program may use at most 64 MiB of HBM per device.

v0:
```python
import functools

import jax
import jax.numpy as jnp
from jax import lax
from jax.experimental import pallas as pl
from jax.experimental.pallas import tpu as pltpu
from jax.sharding import PartitionSpec as P

REACH = 2
PIECES = 4
AHEAD = 2
TILE = 512
MESH = pl.DeviceIdType.MESH


def ladder_kernel(blocks, groups, cd_ref, live_ref, amp_ref, int_ref, out_ref, *scratch):
    slots, depth, cols = int_ref.shape
    rows = amp_ref.shape[1]
    halves = groups // 2
    owned = rows // groups
    piece = owned // PIECES
    steps = halves * PIECES
    far_steps = steps - PIECES
    window = 2 * REACH + 1
    near = scratch[:steps]
    (cd_smem, live_smem, table_sem, weights, own, pair_out, pair_in, far_out, far_in,
     amp_sem, int_sem, amp_send, amp_recv, pair_send, pair_recv, far_send, far_recv) = scratch[steps:]

    here = lax.axis_index("blk")
    me = lax.axis_index("grp")
    half, core = me // 2, me % 2
    mate = half * 2 + 1 - core
    side = 1 - 2 * (here % 2)
    twin = here + side

    amp_loads = []
    for step in range(steps):
        there = (half + step // PIECES + 1) % halves
        for part, lane in enumerate((1 - core, core)):
            start = pl.multiple_of((there * 2 + lane) * owned + (step % PIECES) * piece, piece)
            amp_loads.append(pltpu.make_async_copy(
                amp_ref.at[0, pl.ds(start, piece)],
                near[step].at[REACH, pl.ds(part * piece, piece)],
                amp_sem.at[step, part]))
    int_loads = [pltpu.make_async_copy(int_ref.at[k], weights.at[pl.ds(k * depth, depth)], int_sem.at[k])
                 for k in range(slots)]
    table_loads = [pltpu.make_async_copy(cd_ref, cd_smem, table_sem.at[0]),
                   pltpu.make_async_copy(live_ref, live_smem, table_sem.at[1])]
    for load in amp_loads + int_loads + table_loads:
        load.start()

    up, down = (here + REACH) % blocks, (here - REACH + blocks) % blocks
    barrier = pltpu.get_barrier_semaphore()
    for target in (up, down, twin):
        pl.semaphore_signal(barrier, inc=1, device_id={"blk": target}, device_id_type=MESH)
    pl.semaphore_signal(barrier, inc=1, device_id={"grp": mate}, device_id_type=MESH)
    for hop in range(1, halves):
        pl.semaphore_signal(barrier, inc=1, device_id={"grp": (half + hop) % halves * 2 + core}, device_id_type=MESH)
    for step in range(steps):
        near[step][window] = jnp.zeros(near[step].shape[1:], near[step].dtype)
    for load in amp_loads:
        load.wait()
    pl.semaphore_wait(barrier, 3 + halves)

    def push(step, source, slot, lane, target):
        return pltpu.make_async_remote_copy(
            near[step].at[source], near[step].at[slot], amp_send.at[lane, step], amp_recv.at[slot, step],
            device_id={"blk": target}, device_id_type=MESH)

    def arrival(step, slot):
        push(step, REACH, slot, 0, up).wait_recv()

    sent = []

    def launch(copy):
        copy.start()
        sent.append(copy)

    def push_twin(step):
        if step < steps:
            launch(push(step, REACH, REACH - side, 2, twin))

    def forward(step):
        if step < steps:
            arrival(step, REACH + 2 * side)
            launch(push(step, REACH + 2 * side, REACH + side, 3, twin))
            push_twin(step + AHEAD)

    for step in range(steps):
        launch(push(step, REACH, 0, 0, up))
        launch(push(step, REACH, 2 * REACH, 1, down))
        if step < AHEAD:
            push_twin(step)

    for load in table_loads:
        load.wait()
    picks = []
    for k in range(slots):
        offset = (cd_smem[here * slots + k] - here + REACH + blocks) % blocks
        picks.append(jnp.where(k < live_smem[here], offset, window))

    pair_copies, far_copies = [], []

    def settle(step):
        pair_copies[step].wait_recv()
        if step < far_steps:
            far_out[step] = own[step] + pair_in[step]
            there = (half + step // PIECES + 1) % halves * 2 + core
            copy = pltpu.make_async_remote_copy(
                far_out.at[step], far_in.at[step], far_send.at[step], far_recv.at[step],
                device_id={"grp": there}, device_id_type=MESH)
            copy.start()
            far_copies.append(copy)

    for load in int_loads:
        load.wait()
    forward(0)
    for step in range(steps):
        forward(step + 1)
        for slot in (REACH - 2 * side, REACH - side, REACH + side):
            arrival(step, slot)
        lhs = jnp.concatenate([near[step][pick] for pick in picks], axis=1)

        @pl.loop(0, cols // TILE)
        def _(tile):
            lanes = pl.ds(pl.multiple_of(tile * TILE, TILE), TILE)
            product = jnp.dot(lhs, weights[:, lanes], preferred_element_type=jnp.float32)
            pair_out[step, :, lanes] = product[:piece]
            own[step, :, lanes] = product[piece:]

        copy = pltpu.make_async_remote_copy(
            pair_out.at[step], pair_in.at[step], pair_send.at[step], pair_recv.at[step],
            device_id={"grp": mate}, device_id_type=MESH)
        copy.start()
        pair_copies.append(copy)
        if step >= 1:
            settle(step - 1)
    settle(steps - 1)
    for part in range(PIECES):
        total = own[far_steps + part] + pair_in[far_steps + part]
        for hop in range(halves - 1):
            far_copies[hop * PIECES + part].wait_recv()
            total = total + far_in[hop * PIECES + part]
        out_ref[pl.ds(part * piece, piece)] = total
    for copy in sent + pair_copies + far_copies:
        copy.wait_send()


def body(blocks, groups, amplitudes, integrals, cd_index, live_blocks, occ_energy, vir_energy):
    slots, depth, cols = integrals.shape
    rows = amplitudes.shape[1]
    owned = rows // groups
    piece = owned // PIECES
    steps = groups // 2 * PIECES
    far_steps = steps - PIECES
    window = 2 * REACH + 1
    ladder = pl.pallas_call(
        functools.partial(ladder_kernel, blocks, groups),
        out_shape=jax.ShapeDtypeStruct((owned, cols), jnp.float32),
        in_specs=[pl.BlockSpec(memory_space=pltpu.HBM)] * 4,
        out_specs=pl.BlockSpec(memory_space=pltpu.VMEM),
        scratch_shapes=[pltpu.VMEM((window + 1, 2 * piece, depth), amplitudes.dtype)] * steps + [
            pltpu.SMEM(cd_index.shape, cd_index.dtype),
            pltpu.SMEM(live_blocks.shape, live_blocks.dtype),
            pltpu.SemaphoreType.DMA((2,)),
            pltpu.VMEM((slots * depth, cols), integrals.dtype),
            pltpu.VMEM((steps, piece, cols), jnp.float32),
            pltpu.VMEM((steps, piece, cols), jnp.float32),
            pltpu.VMEM((steps, piece, cols), jnp.float32),
            pltpu.VMEM((far_steps, piece, cols), jnp.float32),
            pltpu.VMEM((far_steps, piece, cols), jnp.float32),
            pltpu.SemaphoreType.DMA((steps, 2)),
            pltpu.SemaphoreType.DMA((slots,)),
            pltpu.SemaphoreType.DMA((4, steps)),
            pltpu.SemaphoreType.DMA((window, steps)),
            pltpu.SemaphoreType.DMA((steps,)),
            pltpu.SemaphoreType.DMA((steps,)),
            pltpu.SemaphoreType.DMA((far_steps,)),
            pltpu.SemaphoreType.DMA((far_steps,)),
        ],
        compiler_params=pltpu.CompilerParams(
            collective_id=0, has_side_effects=True, vmem_limit_bytes=24 * 1024 * 1024),
    )(*[pltpu.with_memory_space_constraint(x, pltpu.HBM) for x in (cd_index, live_blocks, amplitudes, integrals)])
    denominator = vir_energy[0][None, :] - occ_energy[:, None]
    return (ladder / denominator)[None]


def solution(mesh):
    return jax.shard_map(
        functools.partial(body, mesh.shape["blk"], mesh.shape["grp"]),
        mesh=mesh,
        in_specs=(P("blk", None, "grp"), P("blk", "grp", None), P(), P(), P("grp"), P("blk", None)),
        out_specs=P("blk", "grp", None),
        check_vma=False,
    )
```

profile of v0, /device:TPU:0, one launch (start us, length us, event | category | flops | bytes accessed | tf_op | source)
XLA Modules:
  0.0 30.8 jit_solution(13488770267798503212)
XLA Ops:
  0.0 0.0 copy-start
  0.0 0.0 copy-start.1
  0.0 29.8 %shard_map.64 = f32[128,1024]{1,0:T(8,128)S(1)} custom-call(s32[64]{0:T(128)} %cd_ref.1, s32[8]{0:T(128)} %live_ref.1, bf16[1,512,256]{2,1,0:T(8,128)(2,1)} %amp_ref.1, bf16[8,256,1024]{2,1,0:T(8,128)(2,1)} %int_ref.1), custom_call_target="tpu_custom_call" | custom-call | tf_op jit(solution)/shard_map/pallas_call | solution.py:158
  29.8 0.0 copy-done
  29.8 0.0 copy-done.1
  29.8 0.9 %divide_bitcast_fusion = f32[1,128,1024]{2,1,0:T(8,128)} fusion(f32[128,1024]{1,0:T(8,128)S(1)} %shard_map.64, f32[128]{0:T(128)S(1)} %copy-done.1, f32[1024]{0:T(1024)S(1)} %bitcast.3), kind=kLoop, calls=%fused_computation | loop fusion | flops 262144 | bytes 1053184 | tf_op jit(solution)/shard_map/broadcast_in_dim | solution.py:186
Async XLA Ops:
  0.0 29.8 %copy-start = (f32[1,1024]{1,0:T(1,128)S(1)}, f32[1,1024]{1,0:T(1,128)}, u32[]{:S(2)}) copy-start(f32[1,1024]{1,0:T(1,128)} %param.11) | copy-start | bytes 12292
  0.0 29.8 %copy-start.1 = (f32[128]{0:T(128)S(1)}, f32[128]{0:T(128)}, u32[]{:S(2)}) copy-start(f32[128]{0:T(128)} %param.10) | copy-start | bytes 1540
where the time goes:
time: 30.9 us; the launch traced here: 30.8 us
  Pallas kernels  29.8 us (96%)
  other arithmetic  0.94 us (3%)
    pallas_call x1, Pallas kernels, body(): pl.pallas_call(functools.partial(ladder_kernel, blocks, groups), out_shap...  29.8 us
    broadcast_in_dim x1, other arithmetic, body(): return (ladder / denominator)[None]  0.94 us

commit v1 on v0

v1 whole, which is shorter than its diff:
```python
import functools

import jax
import jax.numpy as jnp
from jax import lax
from jax.experimental import pallas as pl
from jax.experimental.pallas import tpu as pltpu
from jax.sharding import PartitionSpec as P

REACH = 2
FAR = (4, 4, 4, 4)
NEAR = (4, 4, 4, 4)
LEAD = 3
AHEAD = 5
LOOK = 2
TILE = 512
MESH = pl.DeviceIdType.MESH
COMPUTE, MATE, YEX, AMP = True, True, True, True
LANES = 128
TOP = 32760.0


def plan(rows, groups):
    owned = rows // groups
    hops = groups // 2
    far = [owned * p // sum(FAR) for p in FAR]
    near = [owned * p // sum(NEAR) for p in NEAR]
    out = []
    for hop in range(1, hops + 1):
        at = 0
        for piece in (far if hop < hops else near):
            out.append((hop % hops, at, piece))
            at += piece
    return out


def ladder_kernel(blocks, groups, cd_ref, live_ref, amp_ref, int_ref, out_ref, *scratch):
    slots, depth, cols = int_ref.shape
    rows = amp_ref.shape[1]
    halves = groups // 2
    owned = rows // groups
    chunks = plan(rows, groups)
    steps = len(chunks)
    far_steps = sum(1 for c in chunks if c[0])
    window = 2 * REACH + 1
    near, own, pair_out, pair_in = (scratch[i * steps:(i + 1) * steps] for i in range(4))
    rest = scratch[4 * steps:]
    far_out, far_in = rest[:far_steps], rest[far_steps:2 * far_steps]
    (cd_smem, live_smem, table_sem, weights, peak_out, peak_in, amp_sem, int_sem, amp_send, amp_recv,
     pair_send, pair_recv, far_send, far_recv) = rest[2 * far_steps:]

    here = lax.axis_index("blk")
    me = lax.axis_index("grp")
    half, core = me // 2, me % 2
    mate = half * 2 + 1 - core
    side = 1 - 2 * (here % 2)
    twin = here + side
    ahead, behind = (here + 2 * side + blocks) % blocks, (here - 2 * side + blocks) % blocks

    amp_loads = []
    for step, (hop, at, piece) in enumerate(chunks):
        there = (half + hop) % halves
        for part, lane in enumerate((1 - core, core)):
            start = pl.multiple_of((there * 2 + lane) * owned + at, 16)
            amp_loads.append(pltpu.make_async_copy(
                amp_ref.at[0, pl.ds(start, piece)],
                near[step].at[REACH, pl.ds(part * piece, piece)],
                amp_sem.at[step, part]))
    int_loads = [pltpu.make_async_copy(int_ref.at[k], weights.at[pl.ds(k * depth, depth)], int_sem.at[k])
                 for k in range(slots)]
    table_loads = [pltpu.make_async_copy(cd_ref, cd_smem, table_sem.at[0]),
                   pltpu.make_async_copy(live_ref, live_smem, table_sem.at[1])]
    for load in amp_loads:
        load.start()

    barrier = pltpu.get_barrier_semaphore()
    for target in (ahead, behind, twin):
        pl.semaphore_signal(barrier, inc=1, device_id={"blk": target}, device_id_type=MESH)
    pl.semaphore_signal(barrier, inc=1, device_id={"grp": mate}, device_id_type=MESH)
    for hop in range(1, halves):
        pl.semaphore_signal(barrier, inc=1, device_id={"grp": (half + hop) % halves * 2 + core}, device_id_type=MESH)
    for load in table_loads:
        load.start()
    pl.semaphore_wait(barrier, 3 + halves)

    def push(step, source, slot, lane, target):
        return pltpu.make_async_remote_copy(
            near[step].at[source], near[step].at[slot], amp_send.at[lane, step], amp_recv.at[slot, step],
            device_id={"blk": target}, device_id_type=MESH)

    def arrival(step, slot):
        if AMP:
            push(step, REACH, slot, 0, twin).wait_recv()

    sent = []

    def launch(copy):
        if AMP:
            copy.start()
            sent.append(copy)

    def push_passed(step):
        if step < steps:
            launch(push(step, REACH, REACH + 2 * side, 0, behind))

    def push_kept(step):
        if 0 <= step < steps:
            launch(push(step, REACH, REACH - 2 * side, 1, ahead))

    def push_twin(step):
        if step < steps:
            launch(push(step, REACH, REACH - side, 2, twin))

    def forward(step):
        if step < steps:
            arrival(step, REACH + 2 * side)
            launch(push(step, REACH + 2 * side, REACH + side, 3, twin))
            push_twin(step + AHEAD)

    for step in range(steps + LEAD):
        if step < steps:
            amp_loads[2 * step].wait()
            amp_loads[2 * step + 1].wait()
            push_passed(step)
            if step < AHEAD:
                push_twin(step)
        push_kept(step - LEAD)
    for load in int_loads:
        load.start()
    for step in range(steps):
        near[step][window] = jnp.zeros(near[step].shape[1:], near[step].dtype)

    for load in table_loads:
        load.wait()
    picks = []
    for k in range(slots):
        offset = (cd_smem[here * slots + k] - here + REACH + blocks) % blocks
        picks.append(jnp.where(k < live_smem[here], offset, window))

    pair_copies, far_copies = [], []

    def settle(step):
        hop, at, piece = chunks[step]
        if MATE:
            pair_copies[step].wait_recv()
        total = own[step][...] + pair_in[step][...]
        if hop:
            tiles = [total[:, j:j + LANES].reshape(piece // 8, 8, LANES) for j in range(0, cols, LANES)]
            peak = functools.reduce(jnp.maximum, [jnp.max(jnp.abs(t), axis=0) for t in tiles])
            peak = jnp.maximum(peak, 1e-30)
            peak_out[step] = peak * (1 / TOP)
            for j, t in enumerate(tiles):
                code = jnp.round(t * (TOP / peak)[None]).astype(jnp.int32).astype(jnp.int16)
                far_out[step][:, j * LANES:(j + 1) * LANES] = code.reshape(piece, LANES)
            there = (half + hop) % halves * 2 + core
            pair = [pltpu.make_async_remote_copy(
                source, target, far_send.at[kind, step], far_recv.at[kind, step],
                device_id={"grp": there}, device_id_type=MESH)
                for kind, (source, target) in enumerate(((far_out[step], far_in[step]), (peak_out.at[step], peak_in.at[step])))]
            if YEX:
                for copy in pair:
                    copy.start()
                far_copies.append(pair)
        else:
            out_ref[pl.ds(at, piece)] = total

    for step in range(LOOK):
        forward(step)
    for load in int_loads:
        load.wait()
    for step in range(steps):
        piece = chunks[step][2]
        forward(step + LOOK)
        for slot in (REACH - 2 * side, REACH + side, REACH - side):
            arrival(step, slot)
        if COMPUTE:
            lhs = jnp.concatenate([near[step][pick] for pick in picks], axis=1)

            @pl.loop(0, cols // TILE)
            def _(tile):
                lanes = pl.ds(pl.multiple_of(tile * TILE, TILE), TILE)
                product = jnp.dot(lhs, weights[:, lanes], preferred_element_type=jnp.float32)
                pair_out[step][:, lanes] = product[:piece]
                own[step][:, lanes] = product[piece:]

        copy = pltpu.make_async_remote_copy(
            pair_out[step], pair_in[step], pair_send.at[step], pair_recv.at[step],
            device_id={"grp": mate}, device_id_type=MESH)
        if MATE:
            copy.start()
            pair_copies.append(copy)
        if step >= 1:
            settle(step - 1)
    settle(steps - 1)
    if YEX:
        for step in range(far_steps):
            hop, at, piece = chunks[step]
            for copy in far_copies[step]:
                copy.wait_recv()
            peak = peak_in[step][None]
            for j in range(0, cols, LANES):
                code = far_in[step][:, j:j + LANES].astype(jnp.int32).astype(jnp.float32)
                value = (code.reshape(piece // 8, 8, LANES) * peak).reshape(piece, LANES)
                out_ref[pl.ds(at, piece), j:j + LANES] = out_ref[pl.ds(at, piece), j:j + LANES] + value
    for copy in sent + pair_copies + [copy for pair in far_copies for copy in pair]:
        copy.wait_send()


def body(blocks, groups, amplitudes, integrals, cd_index, live_blocks, occ_energy, vir_energy):
    slots, depth, cols = integrals.shape
    rows = amplitudes.shape[1]
    owned = rows // groups
    chunks = plan(rows, groups)
    steps = len(chunks)
    far = [c for c in chunks if c[0]]
    window = 2 * REACH + 1
    f32 = [pltpu.VMEM((c[2], cols), jnp.float32) for c in chunks]
    i16 = [pltpu.VMEM((c[2], cols), jnp.int16) for c in far]
    ladder = pl.pallas_call(
        functools.partial(ladder_kernel, blocks, groups),
        out_shape=jax.ShapeDtypeStruct((owned, cols), jnp.float32),
        in_specs=[pl.BlockSpec(memory_space=pltpu.HBM)] * 4,
        out_specs=pl.BlockSpec(memory_space=pltpu.VMEM),
        scratch_shapes=[pltpu.VMEM((window + 1, 2 * c[2], depth), amplitudes.dtype) for c in chunks] + f32 * 3 + i16 * 2 + [
            pltpu.SMEM(cd_index.shape, cd_index.dtype),
            pltpu.SMEM(live_blocks.shape, live_blocks.dtype),
            pltpu.SemaphoreType.DMA((2,)),
            pltpu.VMEM((slots * depth, cols), integrals.dtype),
            pltpu.VMEM((len(far), 8, LANES), jnp.float32),
            pltpu.VMEM((len(far), 8, LANES), jnp.float32),
            pltpu.SemaphoreType.DMA((steps, 2)),
            pltpu.SemaphoreType.DMA((slots,)),
            pltpu.SemaphoreType.DMA((4, steps)),
            pltpu.SemaphoreType.DMA((window, steps)),
            pltpu.SemaphoreType.DMA((steps,)),
            pltpu.SemaphoreType.DMA((steps,)),
            pltpu.SemaphoreType.DMA((2, len(far))),
            pltpu.SemaphoreType.DMA((2, len(far))),
        ],
        compiler_params=pltpu.CompilerParams(
            collective_id=0, has_side_effects=True, vmem_limit_bytes=24 * 1024 * 1024),
    )(*[pltpu.with_memory_space_constraint(x, pltpu.HBM) for x in (cd_index, live_blocks, amplitudes, integrals)])
    denominator = vir_energy[0][None, :] - occ_energy[:, None]
    return (ladder / denominator)[None]


def solution(mesh):
    return jax.shard_map(
        functools.partial(body, mesh.shape["blk"], mesh.shape["grp"]),
        mesh=mesh,
        in_specs=(P("blk", None, "grp"), P("blk", "grp", None), P(), P(), P("grp"), P("blk", None)),
        out_specs=P("blk", "grp", None),
        check_vma=False,
    )
```

time: 30.9 us -> 26.2 us (0.85)
  Pallas kernels: 29.8 us -> 25 us
    pallas_call x1, Pallas kernels: 29.8 us -> 25 us  [body(): pl.pallas_call(functools.partial(ladder_kernel, blocks, groups), out_shap...]
where the time goes in v1:
time: 26.2 us; the launch traced here: 26 us
  Pallas kernels  25 us (95%)
  other arithmetic  0.94 us (4%)
    pallas_call x1, Pallas kernels, body(): pl.pallas_call(functools.partial(ladder_kernel, blocks, groups), out_shap...  25 us
    broadcast_in_dim x1, other arithmetic, body(): return (ladder / denominator)[None]  0.94 us

profile of v1, /device:TPU:0, one launch (start us, length us, event | category | flops | bytes accessed | tf_op | source)
XLA Modules:
  0.0 26.0 jit_solution(10554583540010466553)
XLA Ops:
  0.0 0.0 copy-start
  0.0 0.0 copy-start.1
  0.0 25.0 %shard_map.64 = f32[128,1024]{1,0:T(8,128)S(1)} custom-call(s32[64]{0:T(128)} %cd_ref.1, s32[8]{0:T(128)} %live_ref.1, bf16[1,512,256]{2,1,0:T(8,128)(2,1)} %amp_ref.1, bf16[8,256,1024]{2,1,0:T(8,128)(2,1)} %int_ref.1), custom_call_target="tpu_custom_call" | custom-call | tf_op jit(solution)/shard_map/pallas_call | solution.py:219
  25.0 0.0 copy-done
  25.1 0.0 copy-done.1
  25.1 0.9 %divide_bitcast_fusion = f32[1,128,1024]{2,1,0:T(8,128)} fusion(f32[128,1024]{1,0:T(8,128)S(1)} %shard_map.64, f32[128]{0:T(128)S(1)} %copy-done.1, f32[1024]{0:T(1024)S(1)} %bitcast.3), kind=kLoop, calls=%fused_computation | loop fusion | flops 262144 | bytes 1053184 | tf_op jit(solution)/shard_map/broadcast_in_dim | solution.py:244
Async XLA Ops:
  0.0 25.0 %copy-start = (f32[1,1024]{1,0:T(1,128)S(1)}, f32[1,1024]{1,0:T(1,128)}, u32[]{:S(2)}) copy-start(f32[1,1024]{1,0:T(1,128)} %param.11) | copy-start | bytes 12292
  0.0 25.1 %copy-start.1 = (f32[128]{0:T(128)S(1)}, f32[128]{0:T(128)}, u32[]{:S(2)}) copy-start(f32[128]{0:T(128)} %param.10) | copy-start | bytes 1540

commit v2 on v1

--- a/solution.py
+++ b/solution.py
@@ -10,12 +10,10 @@
 REACH = 2
 FAR = (4, 4, 4, 4)
 NEAR = (4, 4, 4, 4)
-LEAD = 3
-AHEAD = 5
-LOOK = 2
-TILE = 512
+LEAD = 4
+AHEAD = 4
+LOOK = 3
 MESH = pl.DeviceIdType.MESH
-COMPUTE, MATE, YEX, AMP = True, True, True, True
 LANES = 128
 TOP = 32760.0
 
@@ -81,6 +79,8 @@
         pl.semaphore_signal(barrier, inc=1, device_id={"grp": (half + hop) % halves * 2 + core}, device_id_type=MESH)
     for load in table_loads:
         load.start()
+    for step in range(steps):
+        near[step][window] = jnp.zeros(near[step].shape[1:], near[step].dtype)
     pl.semaphore_wait(barrier, 3 + halves)
 
     def push(step, source, slot, lane, target):
@@ -89,15 +89,13 @@
             device_id={"blk": target}, device_id_type=MESH)
 
     def arrival(step, slot):
-        if AMP:
-            push(step, REACH, slot, 0, twin).wait_recv()
+        push(step, REACH, slot, 0, twin).wait_recv()
 
     sent = []
 
     def launch(copy):
-        if AMP:
-            copy.start()
-            sent.append(copy)
+        copy.start()
+        sent.append(copy)
 
     def push_passed(step):
         if step < steps:
@@ -127,8 +125,6 @@
         push_kept(step - LEAD)
     for load in int_loads:
         load.start()
-    for step in range(steps):
-        near[step][window] = jnp.zeros(near[step].shape[1:], near[step].dtype)
 
     for load in table_loads:
         load.wait()
@@ -141,8 +137,7 @@
 
     def settle(step):
         hop, at, piece = chunks[step]
-        if MATE:
-            pair_copies[step].wait_recv()
+        pair_copies[step].wait_recv()
         total = own[step][...] + pair_in[step][...]
         if hop:
             tiles = [total[:, j:j + LANES].reshape(piece // 8, 8, LANES) for j in range(0, cols, LANES)]
@@ -157,10 +152,9 @@
                 source, target, far_send.at[kind, step], far_recv.at[kind, step],
                 device_id={"grp": there}, device_id_type=MESH)
                 for kind, (source, target) in enumerate(((far_out[step], far_in[step]), (peak_out.at[step], peak_in.at[step])))]
-            if YEX:
-                for copy in pair:
-                    copy.start()
-                far_copies.append(pair)
+            for copy in pair:
+                copy.start()
+            far_copies.append(pair)
         else:
             out_ref[pl.ds(at, piece)] = total
 
@@ -173,35 +167,29 @@
         forward(step + LOOK)
         for slot in (REACH - 2 * side, REACH + side, REACH - side):
             arrival(step, slot)
-        if COMPUTE:
-            lhs = jnp.concatenate([near[step][pick] for pick in picks], axis=1)
-
-            @pl.loop(0, cols // TILE)
-            def _(tile):
-                lanes = pl.ds(pl.multiple_of(tile * TILE, TILE), TILE)
-                product = jnp.dot(lhs, weights[:, lanes], preferred_element_type=jnp.float32)
-                pair_out[step][:, lanes] = product[:piece]
-                own[step][:, lanes] = product[piece:]
+        lhs = jnp.concatenate([near[step][pick] for pick in picks], axis=1)
+
+        product = jnp.dot(lhs, weights[...], preferred_element_type=jnp.float32)
+        pair_out[step][...] = product[:piece]
+        own[step][...] = product[piece:]
 
         copy = pltpu.make_async_remote_copy(
             pair_out[step], pair_in[step], pair_send.at[step], pair_recv.at[step],
             device_id={"grp": mate}, device_id_type=MESH)
-        if MATE:
-            copy.start()
-            pair_copies.append(copy)
+        copy.start()
+        pair_copies.append(copy)
         if step >= 1:
             settle(step - 1)
     settle(steps - 1)
-    if YEX:
-        for step in range(far_steps):
-            hop, at, piece = chunks[step]
-            for copy in far_copies[step]:
-                copy.wait_recv()
-            peak = peak_in[step][None]
-            for j in range(0, cols, LANES):
-                code = far_in[step][:, j:j + LANES].astype(jnp.int32).astype(jnp.float32)
-                value = (code.reshape(piece // 8, 8, LANES) * peak).reshape(piece, LANES)
-                out_ref[pl.ds(at, piece), j:j + LANES] = out_ref[pl.ds(at, piece), j:j + LANES] + value
+    for step in range(far_steps):
+        hop, at, piece = chunks[step]
+        for copy in far_copies[step]:
+            copy.wait_recv()
+        peak = peak_in[step][None]
+        for j in range(0, cols, LANES):
+            code = far_in[step][:, j:j + LANES].astype(jnp.int32).astype(jnp.float32)
+            value = (code.reshape(piece // 8, 8, LANES) * peak).reshape(piece, LANES)
+            out_ref[pl.ds(at, piece), j:j + LANES] = out_ref[pl.ds(at, piece), j:j + LANES] + value
     for copy in sent + pair_copies + [copy for pair in far_copies for copy in pair]:
         copy.wait_send()
 

time: 26.2 us -> 25.4 us (0.969)
  Pallas kernels: 25 us -> 24.3 us
    pallas_call x1, Pallas kernels: 25 us -> 24.3 us  [body(): pl.pallas_call(functools.partial(ladder_kernel, blocks, groups), out_shap...]
where the time goes in v2:
time: 25.4 us; the launch traced here: 25.2 us
  Pallas kernels  24.3 us (96%)
  other arithmetic  0.94 us (4%)
    pallas_call x1, Pallas kernels, body(): pl.pallas_call(functools.partial(ladder_kernel, blocks, groups), out_shap...  24.3 us
    broadcast_in_dim x1, other arithmetic, body(): return (ladder / denominator)[None]  0.94 us

profile of v2, /device:TPU:0, one launch (start us, length us, event | category | flops | bytes accessed | tf_op | source)
XLA Modules:
  0.0 25.2 jit_solution(14774690644395439651)
XLA Ops:
  0.0 0.0 copy-start
  0.0 0.0 copy-start.1
  0.0 24.3 %shard_map.64 = f32[128,1024]{1,0:T(8,128)S(1)} custom-call(s32[64]{0:T(128)} %cd_ref.1, s32[8]{0:T(128)} %live_ref.1, bf16[1,512,256]{2,1,0:T(8,128)(2,1)} %amp_ref.1, bf16[8,256,1024]{2,1,0:T(8,128)(2,1)} %int_ref.1), custom_call_target="tpu_custom_call" | custom-call | tf_op jit(solution)/shard_map/pallas_call | solution.py:207
  24.3 0.0 copy-done
  24.3 0.0 copy-done.1
  24.3 0.9 %divide_bitcast_fusion = f32[1,128,1024]{2,1,0:T(8,128)} fusion(f32[128,1024]{1,0:T(8,128)S(1)} %shard_map.64, f32[128]{0:T(128)S(1)} %copy-done.1, f32[1024]{0:T(1024)S(1)} %bitcast.3), kind=kLoop, calls=%fused_computation | loop fusion | flops 262144 | bytes 1053184 | tf_op jit(solution)/shard_map/broadcast_in_dim | solution.py:232
Async XLA Ops:
  0.0 24.3 %copy-start = (f32[1,1024]{1,0:T(1,128)S(1)}, f32[1,1024]{1,0:T(1,128)}, u32[]{:S(2)}) copy-start(f32[1,1024]{1,0:T(1,128)} %param.11) | copy-start | bytes 12292
  0.0 24.3 %copy-start.1 = (f32[128]{0:T(128)S(1)}, f32[128]{0:T(128)}, u32[]{:S(2)}) copy-start(f32[128]{0:T(128)} %param.10) | copy-start | bytes 1540

commit v3 on v2

--- a/solution.py
+++ b/solution.py
@@ -10,9 +10,10 @@
 REACH = 2
 FAR = (4, 4, 4, 4)
 NEAR = (4, 4, 4, 4)
-LEAD = 4
+LEAD = 3
 AHEAD = 4
 LOOK = 3
+PACE = 1
 MESH = pl.DeviceIdType.MESH
 LANES = 128
 TOP = 32760.0
@@ -54,6 +55,9 @@
     side = 1 - 2 * (here % 2)
     twin = here + side
     ahead, behind = (here + 2 * side + blocks) % blocks, (here - 2 * side + blocks) % blocks
+
+    low, high = here < 2, here + 2 >= blocks
+    paced = ~low & ~high
 
     amp_loads = []
     for step, (hop, at, piece) in enumerate(chunks):
@@ -93,17 +97,21 @@
 
     sent = []
 
-    def launch(copy):
-        copy.start()
-        sent.append(copy)
+    def launch(copy, when=None, first=True):
+        if when is None:
+            copy.start()
+        else:
+            pl.when(when)(copy.start)
+        if first:
+            sent.append(copy)
 
     def push_passed(step):
         if step < steps:
             launch(push(step, REACH, REACH + 2 * side, 0, behind))
 
-    def push_kept(step):
+    def push_kept(step, when=None, first=True):
         if 0 <= step < steps:
-            launch(push(step, REACH, REACH - 2 * side, 1, ahead))
+            launch(push(step, REACH, REACH - 2 * side, 1, ahead), when, first)
 
     def push_twin(step):
         if step < steps:
@@ -114,6 +122,7 @@
             arrival(step, REACH + 2 * side)
             launch(push(step, REACH + 2 * side, REACH + side, 3, twin))
             push_twin(step + AHEAD)
+            push_kept(step + PACE, paced, False)
 
     for step in range(steps + LEAD):
         if step < steps:
@@ -122,7 +131,7 @@
             push_passed(step)
             if step < AHEAD:
                 push_twin(step)
-        push_kept(step - LEAD)
+        push_kept(step - LEAD, None if step - LEAD < PACE else ~paced)
     for load in int_loads:
         load.start()
 

time: 25.4 us -> 24.8 us (0.976)
  Pallas kernels: 24.3 us -> 23.7 us
    pallas_call x1, Pallas kernels: 24.3 us -> 23.7 us  [body(): pl.pallas_call(functools.partial(ladder_kernel, blocks, groups), out_shap...]
where the time goes in v3:
time: 24.8 us; the launch traced here: 24.7 us
  Pallas kernels  23.7 us (96%)
  other arithmetic  0.94 us (4%)
    pallas_call x1, Pallas kernels, body(): pl.pallas_call(functools.partial(ladder_kernel, blocks, groups), out_shap...  23.7 us
    broadcast_in_dim x1, other arithmetic, body(): return (ladder / denominator)[None]  0.94 us

profile of v3, /device:TPU:0, one launch (start us, length us, event | category | flops | bytes accessed | tf_op | source)
XLA Modules:
  0.0 24.7 jit_solution(2618769508173587297)
XLA Ops:
  0.0 0.0 copy-start
  0.0 0.0 copy-start.1
  0.0 23.7 %shard_map.64 = f32[128,1024]{1,0:T(8,128)S(1)} custom-call(s32[64]{0:T(128)} %cd_ref.1, s32[8]{0:T(128)} %live_ref.1, bf16[1,512,256]{2,1,0:T(8,128)(2,1)} %amp_ref.1, bf16[8,256,1024]{2,1,0:T(8,128)(2,1)} %int_ref.1), custom_call_target="tpu_custom_call" | custom-call | tf_op jit(solution)/shard_map/pallas_call | solution.py:216
  23.7 0.0 copy-done
  23.7 0.0 copy-done.1
  23.7 0.9 %divide_bitcast_fusion = f32[1,128,1024]{2,1,0:T(8,128)} fusion(f32[128,1024]{1,0:T(8,128)S(1)} %shard_map.64, f32[128]{0:T(128)S(1)} %copy-done.1, f32[1024]{0:T(1024)S(1)} %bitcast.3), kind=kLoop, calls=%fused_computation | loop fusion | flops 262144 | bytes 1053184 | tf_op jit(solution)/shard_map/broadcast_in_dim | solution.py:241
Async XLA Ops:
  0.0 23.7 %copy-start = (f32[1,1024]{1,0:T(1,128)S(1)}, f32[1,1024]{1,0:T(1,128)}, u32[]{:S(2)}) copy-start(f32[1,1024]{1,0:T(1,128)} %param.11) | copy-start | bytes 12292
  0.0 23.7 %copy-start.1 = (f32[128]{0:T(128)S(1)}, f32[128]{0:T(128)}, u32[]{:S(2)}) copy-start(f32[128]{0:T(128)} %param.10) | copy-start | bytes 1540

commit v4 on v3

--- a/solution.py
+++ b/solution.py
@@ -11,7 +11,7 @@
 FAR = (4, 4, 4, 4)
 NEAR = (4, 4, 4, 4)
 LEAD = 3
-AHEAD = 4
+AHEAD = 3
 LOOK = 3
 PACE = 1
 MESH = pl.DeviceIdType.MESH

time: 24.8 us -> 24.8 us (level)
  no operation moved by 1% of the time
where the time goes in v4:
time: 24.8 us; the launch traced here: 24.7 us
  Pallas kernels  23.7 us (96%)
  other arithmetic  0.94 us (4%)
    pallas_call x1, Pallas kernels, body(): pl.pallas_call(functools.partial(ladder_kernel, blocks, groups), out_shap...  23.7 us
    broadcast_in_dim x1, other arithmetic, body(): return (ladder / denominator)[None]  0.94 us

profile of v4, /device:TPU:0, one launch (start us, length us, event | category | flops | bytes accessed | tf_op | source)
XLA Modules:
  0.0 24.7 jit_solution(11113598792207119590)
XLA Ops:
  0.0 0.0 copy-start
  0.0 0.0 copy-start.1
  0.0 23.7 %shard_map.64 = f32[128,1024]{1,0:T(8,128)S(1)} custom-call(s32[64]{0:T(128)} %cd_ref.1, s32[8]{0:T(128)} %live_ref.1, bf16[1,512,256]{2,1,0:T(8,128)(2,1)} %amp_ref.1, bf16[8,256,1024]{2,1,0:T(8,128)(2,1)} %int_ref.1), custom_call_target="tpu_custom_call" | custom-call | tf_op jit(solution)/shard_map/pallas_call | solution.py:216
  23.7 0.0 copy-done
  23.7 0.0 copy-done.1
  23.7 0.9 %divide_bitcast_fusion = f32[1,128,1024]{2,1,0:T(8,128)} fusion(f32[128,1024]{1,0:T(8,128)S(1)} %shard_map.64, f32[128]{0:T(128)S(1)} %copy-done.1, f32[1024]{0:T(1024)S(1)} %bitcast.3), kind=kLoop, calls=%fused_computation | loop fusion | flops 262144 | bytes 1053184 | tf_op jit(solution)/shard_map/broadcast_in_dim | solution.py:241
Async XLA Ops:
  0.0 23.7 %copy-start = (f32[1,1024]{1,0:T(1,128)S(1)}, f32[1,1024]{1,0:T(1,128)}, u32[]{:S(2)}) copy-start(f32[1,1024]{1,0:T(1,128)} %param.11) | copy-start | bytes 12292
  0.0 23.7 %copy-start.1 = (f32[128]{0:T(128)S(1)}, f32[128]{0:T(128)}, u32[]{:S(2)}) copy-start(f32[128]{0:T(128)} %param.10) | copy-start | bytes 1540
